TPU v7x, 32 devices: a whole 2x2x4 slice. The times are simulated.
32 devices in a mesh: cells: 8 (over y, x, core), wells: 4 (over z).
Axes of the slice: x: 2, y: 2, z: 4, core: 2. Of those that a mesh axis runs over, the one named last changes fastest.
Arguments:
- cell_state: float32 [3, 4, 131072], P(None, 'wells', 'cells'), may hold values from -6 to 6
- cell_residual: float32 [3, 4, 131072], P(None, 'wells', 'cells'), may hold values from -6 to 6
- cell_block: float32 [9, 4, 131072], P(None, 'wells', 'cells'), may hold values from -4 to 4
- block_inverse: float32 [9, 4, 131072], P(None, 'wells', 'cells'), may hold values from -3.5 to 3.5
- perf_cells: int32 [4, 32, 128], P('wells'), may hold values from 0 to 131071, as said below
- perf_count: int32 [4, 32], P('wells'), may hold values from 32 to 128
- perf_index: float32 [4, 32, 128], P('wells'), may hold values from 0.2 to 2
- seg_parent: int32 [4, 32, 32], P('wells'), may hold values from 0 to 30, as said below
- seg_cond: float32 [4, 32, 32], P('wells'), may hold values from 0.5 to 4
- seg_state: float32 [3, 4, 32, 32], P(None, 'wells'), may hold values from -6 to 6
- seg_source: float32 [3, 4, 32, 32], P(None, 'wells'), may hold values from -6 to 6
Outputs:
- cell_update: float32 [3, 4, 131072], P(None, 'wells', 'cells')
- well_update: float32 [3, 4, 32, 32], P(None, 'wells', 'cells')
- residual_max: float32 [6], replicated
Inputs may be any that keep to these rules, and one draw needn't show every extreme that they name: seg_parent[..., 0] is 0; for s >= 1, seg_parent[..., s] lies between s - 3 and s - 1, so the segments of a well form a tree rooted at segment 0. `perf_cells`: in each region, take the wells in groups of 4 consecutive wells and the cells in blocks of 16384 consecutive cells; exactly 64 slots of each group, live or not, name a cell of each block.
All inputs are finite; a program needn't handle non-finite values.
Results may differ from a plain program's by a relative error of at most 0.0001.
Values sent between devices are 32-bit elements; how exact they have to be, the bound alone decides.
A program may use at most 128 MiB of HBM per device.

v0:
```python
import jax
import jax.numpy as jnp
from jax import lax
from jax.sharding import PartitionSpec as P


def expand_segments(values, slots):
    repeat = slots // values.shape[-1]
    wide = jnp.broadcast_to(values[..., None], values.shape + (repeat,))
    return wide.reshape(values.shape[:-1] + (slots,))


def segment_sums(values, segs):
    return jnp.sum(values.reshape(values.shape[:-1] + (segs, values.shape[-1] // segs)), axis=-1)


def perf_terms(jac_at, state_at, weight, seg_values):
    slots = weight.shape[-1]
    blocks = jac_at.reshape((3, 3) + weight.shape)
    kmat = jnp.sum(blocks[:, None] * blocks[None, :], axis=2)
    kmat = (kmat + jnp.eye(3, dtype=jnp.float32)[:, :, None, None]) * weight[None, None]
    differ = state_at - expand_segments(seg_values, slots)
    flow = jnp.sum(kmat * differ[None], axis=1)
    return (kmat, flow)


def solve_wells(ksum, rsum, parent, cond):
    segs = parent.shape[-1]
    count = parent.shape[0]
    index = jnp.arange(segs, dtype=jnp.int32)
    link = (parent[:, :, None] == index[None, None, :]) & (index[None, :, None] >= 1)
    adjacent = jnp.where(link, cond[:, :, None], jnp.float32(0.0))
    symmetric = adjacent + jnp.swapaxes(adjacent, 1, 2)
    eye_seg = jnp.eye(segs, dtype=jnp.float32)
    matrix = jnp.sum(symmetric, axis=2)[:, :, None] * eye_seg[None] - symmetric + eye_seg[None]
    eye_comp = jnp.eye(3, dtype=jnp.float32)
    blocks = jnp.transpose(ksum, (2, 3, 0, 1))
    dense = (
        matrix[:, :, None, :, None] * eye_comp[None, None, :, None, :]
        + blocks[:, :, :, None, :] * eye_seg[None, :, None, :, None]
    )
    dense = dense.reshape(count, 3 * segs, 3 * segs)
    rhs = jnp.transpose(rsum, (1, 2, 0)).reshape(count, 3 * segs)
    lower = jnp.linalg.cholesky(dense)

    def one_well(low, vec):
        return jax.scipy.linalg.cho_solve((low, True), vec)

    solved = jax.vmap(one_well)(lower, rhs)
    return jnp.transpose(solved.reshape(count, segs, 3), (2, 0, 1))


def on_device(
    cell_state,
    cell_residual,
    cell_block,
    block_inverse,
    perf_cells,
    perf_count,
    perf_index,
    seg_parent,
    seg_cond,
    seg_state,
    seg_source,
):
    shard_cells = cell_state.shape[2]
    region_wells = perf_cells.shape[1]
    slots = perf_cells.shape[2]
    segs = seg_parent.shape[2]
    ncells = lax.axis_size("cells")
    me = lax.axis_index("cells")
    owned = region_wells // ncells
    first = me * owned
    state = cell_state[:, 0]
    resid = cell_residual[:, 0]
    start = me * shard_cells
    offset = perf_cells[0] - start
    inside = (offset >= 0) & (offset < shard_cells)
    safe = jnp.clip(offset, 0, shard_cells - 1)
    live = jnp.arange(slots, dtype=jnp.int32)[None, :] < perf_count[0][:, None]
    weight = jnp.where(inside & live, perf_index[0], jnp.float32(0.0))
    jac_at = cell_block[:, 0][:, safe]
    state_at = state[:, safe]
    kmat, flow = perf_terms(jac_at, state_at, weight, seg_state[:, 0])
    table = jnp.concatenate([kmat.reshape(9, region_wells, slots), flow], axis=0)
    table = segment_sums(table, segs)
    summed = lax.psum_scatter(table, "cells", scatter_dimension=1, tiled=True)
    parent = lax.dynamic_slice_in_dim(seg_parent[0], first, owned, 0)
    cond = lax.dynamic_slice_in_dim(seg_cond[0], first, owned, 0)
    source = lax.dynamic_slice_in_dim(seg_source[:, 0], first, owned, 1)
    wells_here = summed.shape[1]
    ksum = summed[:9].reshape(3, 3, wells_here, segs)
    rsum = summed[9:] + source
    solved = solve_wells(ksum, rsum, parent, cond)
    well_max = jnp.max(jnp.abs(rsum), axis=(1, 2))
    every_well = lax.all_gather(solved, "cells", axis=1, tiled=True)
    spread = expand_segments(every_well, slots)
    delta = jnp.sum(kmat * spread[None], axis=1)
    correction = (
        jnp.zeros((3, shard_cells), jnp.float32).at[:, safe.reshape(-1)].add(delta.reshape(3, -1))
    )
    corrected = resid - correction
    cell_max = jnp.max(jnp.abs(corrected), axis=1)
    cell_top, well_top = lax.pmax((cell_max, well_max), ("cells", "wells"))
    scale = 1.0 / jnp.maximum(jnp.float32(1.0), cell_top)
    inverse = block_inverse[:, 0].reshape(3, 3, shard_cells)
    step = jnp.sum(inverse * corrected[None], axis=1) * scale[:, None]
    residual_max = jnp.concatenate([cell_top, well_top])
    return (step[:, None], solved[:, None], residual_max)


def solution(mesh):
    in_specs = (
        P(None, "wells", "cells"),
        P(None, "wells", "cells"),
        P(None, "wells", "cells"),
        P(None, "wells", "cells"),
        P("wells", None, None),
        P("wells", None),
        P("wells", None, None),
        P("wells", None, None),
        P("wells", None, None),
        P(None, "wells", None, None),
        P(None, "wells", None, None),
    )
    out_specs = (P(None, "wells", "cells"), P(None, "wells", "cells", None), P())
    return jax.shard_map(
        on_device, mesh=mesh, in_specs=in_specs, out_specs=out_specs, check_vma=False
    )
```

profile of v0, /device:TPU:0, one launch (start us, length us, event | category | flops | bytes accessed | tf_op | source)
XLA Modules:
  0.0 272.5 jit_solution(10672945761370054616)
XLA Ops:
  0.7 0.8 fusion.23
  1.5 6.1 %copy.131 = f32[9,1,16384]{0,2,1:T(8,128)} copy(f32[9,1,16384]{2,1,0:T(1,128)} %param.13) | data formatting | bytes 1179648 | tf_op args[2]
  7.5 14.2 %gather_fusion = f32[4096,9]{1,0:T(8,128)S(1)} fusion(f32[9,16384]{0,1:T(8,128)} %bitcast.90, s32[4096]{0:T(1024)S(1)} %get-tuple-element.27), kind=kCustom, calls=%fused_computation | custom fusion | bytes 311296 | tf_op jit(solution)/shard_map/gather | solution.py:82
  21.7 0.6 copy.132
  22.5 4.6 %copy.138 = f32[3,1,16384]{0,2,1:T(8,128)} copy(f32[3,1,16384]{2,1,0:T(1,128)S(1)} %copy-done.3) | data formatting | bytes 393216 | tf_op args[0]
  27.1 17.5 %gather_fusion.1 = f32[4096,3]{1,0:T(8,128)} fusion(f32[3,16384]{0,1:T(8,128)} %bitcast.91, s32[4096]{0:T(1024)S(1)} %get-tuple-element.27), kind=kCustom, calls=%fused_computation.1 | custom fusion | bytes 114688 | tf_op jit(solution)/shard_map/gather | solution.py:83
  45.2 1.9 sub.50
  47.2 0.6 copy.140
  48.9 0.6 maximum_reduce_fusion
  49.6 27.8 %all-reduce = f32[12,32,32]{2,1,0:T(8,128)S(1)} all-reduce(f32[12,32,32]{2,1,0:T(8,128)S(1)} %copy.142), channel_id=2, replica_groups=mesh['cells'=8,'wells'=4] {'cells'}, use_global_device_ids=true, to_apply=%region_4.5.clone | all-reduce | flops 12288 | bytes 98304
  77.4 0.6 dynamic-slice.3
  78.9 3.1 %mul.160 = f32[4,32,3,32,3]{4,3,2,1,0:T(8,128)} broadcast(f32[4,32,3,3]{3,2,1,0:T(4,128)S(1)} %copy.143), dimensions={0,1,2,4} | broadcast | bytes 152064 | tf_op jit(solution)/shard_map/mul | solution.py:40
  82.0 6.5 %mul.161 = f32[4,96,96]{2,1,0:T(8,128)S(1)} reshape(f32[4,32,3,32,3]{4,3,2,1,0:T(8,128)} %mul.160) | data formatting | bytes 294912 | tf_op jit(solution)/shard_map/mul | solution.py:40
  88.6 0.7 dynamic-slice_bitcast_fusion.1
  89.3 0.6 fusion.5
  89.9 3.5 %mul.150 = f32[4,32,3,32,3]{4,3,2,1,0:T(8,128)} broadcast(f32[4,32,32]{2,1,0:T(8,128)S(1)} %fusion.5), dimensions={0,1,3} | broadcast | bytes 163840 | tf_op jit(solution)/shard_map/mul | solution.py:39
  93.5 6.5 %mul.151 = f32[4,96,96]{2,1,0:T(8,128)S(1)} reshape(f32[4,32,3,32,3]{4,3,2,1,0:T(8,128)} %mul.150) | data formatting | bytes 294912 | tf_op jit(solution)/shard_map/mul | solution.py:39
  100.3 1.1 mul.153
  101.8 1.1 mul.163
  103.1 35.2 %custom-call.11 = f32[4,96,96]{2,1,0:T(8,128)S(1)} custom-call(f32[4,96,96]{2,1,0:T(8,128)S(1)} %fusion.9), custom_call_target="Cholesky" | custom-call | tf_op jit(solution)/shard_map/jit(cholesky)/cholesky | solution.py:44
  138.6 29.7 %custom-call.12 = f32[4,1,96,96]{2,3,1,0:T(8,128)S(1)} custom-call(f32[4,1,96,96]{3,2,1,0:T(8,128)S(1)} %select_bitcast_fusion), custom_call_target="InvertDiagBlocksLowerTriangular" | custom-call | tf_op jit(solution)/shard_map/vmap(jit(_cho_solve))/triangular_solve | solution.py:47
  168.3 0.8 abs_reduce_fusion.1
  170.3 8.4 %all_gather.3 = f32[3,32,32]{2,0,1:T(4,128)S(1)} all-gather(f32[3,4,32]{2,0,1:T(4,128)S(1)} %copy.148), channel_id=1, replica_groups=mesh['cells'=8,'wells'=4] {'cells'}, dimensions={1}, use_global_device_ids=true | all-gather | bytes 13824 | tf_op jit(solution)/shard_map/all_gather | solution.py:96
  179.1 0.6 copy.153
  179.8 29.1 %scatter_custom_fusion = f32[3,16384]{0,1:T(8,128)} fusion(s32[4096]{0:T(1024)S(1)} %bitcast.108, f32[4096,3]{1,0:T(8,128)S(1)} %copy.153, f32[]{:T(128)} %constant.69.clone.1), kind=kCustom, calls=%fused_computation.6 | custom fusion | flops 12288 | bytes 196612 | tf_op jit(solution)/shard_map/scatter-add | solution.py:100
  208.9 4.6 %copy.130 = f32[3,1,16384]{0,2,1:T(8,128)} copy(f32[3,1,16384]{2,1,0:T(1,128)S(1)} %copy-done.4) | data formatting | bytes 393216 | tf_op args[1]
  213.5 9.7 %abs_reduce_fusion = (f32[3]{0:T(128)S(1)}, f32[3,16384]{0,1:T(8,128)}) fusion(f32[3,16384]{0,1:T(8,128)} %scatter_custom_fusion, f32[3,1,16384]{0,2,1:T(8,128)} %copy.130), kind=kLoop, calls=%fused_computation.5 | loop fusion | flops 147453 | bytes 589836 | tf_op jit(solution)/shard_map/reduce_max | solution.py:103
  223.2 39.4 %all-reduce.1 = (f32[3]{0:T(128)S(1)}, f32[3]{0:T(128)S(1)}) all-reduce(f32[3]{0:T(128)S(1)} %get-tuple-element.23, f32[3]{0:T(128)S(1)} %get-tuple-element.29), channel_id=1, replica_groups=mesh['cells'=8,'wells'=4] {'cells','wells'}, use_global_device_ids=true, to_apply=%region_11.12 | all-reduce | flops 6 | bytes 48 | tf_op jit(solution)/shard_map/pmax | solution.py:104
  263.2 5.4 %copy.154 = f32[3,16384]{1,0:T(4,128)S(1)} copy(f32[3,16384]{0,1:T(8,128)} %get-tuple-element.24) | data formatting | bytes 393216 | tf_op jit(solution)/shard_map/sub | solution.py:102
  268.6 1.4 reduce.6
  270.9 0.9 reshape_multiply_fusion
  271.8 0.7 copy.155
  (70 shorter events, 6.4 us)
Async XLA Ops:
  0.6 88.0 %copy-start = (f32[1,32,32]{2,1,0:T(8,128)S(1)}, f32[1,32,32]{2,1,0:T(8,128)}, u32[]{:S(2)}) copy-start(f32[1,32,32]{2,1,0:T(8,128)} %param.19) | copy-start | bytes 12292
  0.6 21.7 %copy-start.5 = (s32[1,32,128]{2,1,0:T(8,128)S(1)}, s32[1,32,128]{2,1,0:T(8,128)}, u32[]{:S(2)}) copy-start(s32[1,32,128]{2,1,0:T(8,128)} %param.15) | copy-start | bytes 49156
  0.7 21.7 %copy-start.8 = (s32[1,32]{1,0:T(1,128)S(1)}, s32[1,32]{1,0:T(1,128)}, u32[]{:S(2)}) copy-start(s32[1,32]{1,0:T(1,128)} %param.16) | copy-start | bytes 388
  0.7 21.7 %copy-start.6 = (f32[1,32,128]{2,1,0:T(8,128)S(1)}, f32[1,32,128]{2,1,0:T(8,128)}, u32[]{:S(2)}) copy-start(f32[1,32,128]{2,1,0:T(8,128)} %param.17) | copy-start | bytes 49156
  0.7 21.8 %copy-start.3 = (f32[3,1,16384]{2,1,0:T(1,128)S(1)}, f32[3,1,16384]{2,1,0:T(1,128)}, u32[]{:S(2)}) copy-start(f32[3,1,16384]{2,1,0:T(1,128)} %param.11) | copy-start | bytes 589828
  7.5 37.1 %copy-start.7 = (f32[3,1,32,32]{3,2,1,0:T(8,128)S(1)}, f32[3,1,32,32]{3,2,1,0:T(8,128)}, u32[]{:S(2)}) copy-start(f32[3,1,32,32]{3,2,1,0:T(8,128)} %param.20) | copy-start | bytes 36868
  27.1 50.3 %copy-start.9 = (u32[32]{0:T(128)S(1)}, u32[32]{0:T(128)}, u32[]{:S(2)}) copy-start(u32[32]{0:T(128)} %constant.96) | copy-start | bytes 388
  101.7 107.1 %copy-start.4 = (f32[3,1,16384]{2,1,0:T(1,128)S(1)}, f32[3,1,16384]{2,1,0:T(1,128)}, u32[]{:S(2)}) copy-start(f32[3,1,16384]{2,1,0:T(1,128)} %param.12) | copy-start | bytes 589828
  213.5 59.0 %copy-start.1 = (f32[1,32,32]{2,1,0:T(8,128)S(1)}, f32[1,32,32]{2,1,0:T(8,128)}, u32[]{:S(2)}) copy-start(f32[1,32,32]{2,1,0:T(8,128)} %param.19) | copy-start | bytes 12292
  223.2 45.4 %copy-start.2 = (f32[9,1,16384]{2,1,0:T(1,128)S(1)}, f32[9,1,16384]{2,1,0:T(1,128)}, u32[]{:S(2)}) copy-start(f32[9,1,16384]{2,1,0:T(1,128)} %param.14) | copy-start | bytes 1769476
where the time goes:
time: 273 us; the launch traced here: 272 us
  other arithmetic  113 us (41%)
  local copies, waits for them, and re-layouts  81.6 us (30%)
  blocking collectives  75.6 us (28%)
    pmax x1, blocking collectives, on_device(): cell_top, well_top = lax.pmax((cell_max, well_max), ('cells', 'wells'))  39.4 us
    another operation x4, other arithmetic, solve_wells(): lower = jnp.linalg.cholesky(dense)  35.4 us
    another operation x3, other arithmetic, one_well(): return jax.scipy.linalg.cho_solve((low, True), vec)  29.8 us
    scatter-add x1, other arithmetic, on_device(): jnp.zeros((3, shard_cells), jnp.float32).at[:, safe.reshape(-1)]  29.1 us
    unnamed x1, blocking collectives  27.8 us
    gather x1, local copies, waits for them, and re-layouts, on_device(): state_at = state[:, safe]  17.5 us
    unnamed x27, local copies, waits for them, and re-layouts  16.8 us
    gather x2, local copies, waits for them, and re-layouts, on_device(): jac_at = cell_block[:, 0][:, safe]  14.8 us

commit v1 on v0

v1 whole, which is shorter than its diff:
```python
import functools

import jax
import jax.numpy as jnp
from jax import lax
from jax.experimental import pallas as pl
from jax.experimental.pallas import tpu as pltpu
from jax.sharding import PartitionSpec as P

MESH = pl.DeviceIdType.MESH
F32 = jnp.float32
BF16 = jnp.bfloat16
LANES = 128


def iota(shape, axis):
    return lax.broadcasted_iota(jnp.int32, shape, axis)


def split3(x):
    high = x.astype(BF16).astype(F32)
    rest = x - high
    mid = rest.astype(BF16).astype(F32)
    return high, mid, rest - mid


def dot(a, b):
    return lax.dot_general(a, b, (((1,), (0,)), ((), ())), preferred_element_type=F32)


def dot_nt(a, b):
    return lax.dot_general(a, b, (((1,), (1,)), ((), ())), preferred_element_type=F32)


def ones_where(cond):
    return jnp.where(cond, F32(1.0), F32(0.0)).astype(BF16)


def invert3(a):
    a00, a01, a02, a11, a12, a22 = a
    q0 = 1.0 / a00
    l1 = a01 * q0
    l2 = a02 * q0
    b11 = a11 - l1 * a01
    b12 = a12 - l1 * a02
    b22 = a22 - l2 * a02
    q1 = 1.0 / b11
    m = b12 * q1
    i22 = 1.0 / (b22 - m * b12)
    i12 = -m * i22
    i11 = q1 - m * i12
    i02 = -(l1 * i12 + l2 * i22)
    i01 = -(l1 * i11 + l2 * i12)
    i00 = q0 - (l1 * i01 + l2 * i02)
    return (i00, i01, i02, i11, i12, i22)


def apply3(a, v):
    a00, a01, a02, a11, a12, a22 = a
    x, y, z = v
    return (
        a00 * x + a01 * y + a02 * z,
        a01 * x + a11 * y + a12 * z,
        a02 * x + a12 * y + a22 * z,
    )


def kernel(
    ncells,
    nwells,
    state_ref,
    resid_ref,
    jac_ref,
    inv_ref,
    cells_ref,
    count_ref,
    index_ref,
    parent_ref,
    cond_ref,
    segstate_ref,
    source_ref,
    step_ref,
    well_ref,
    max_ref,
    feat_scr,
    fold_scr,
    fold_int,
    send_buf,
    recv_buf,
    top_send,
    top_recv,
    send_sem,
    recv_sem,
    top_send_sem,
    top_recv_sem,
):
    me = lax.axis_index("cells")
    region = lax.axis_index("wells")
    peers = [
        (dc, dw) for dc in range(ncells) for dw in range(nwells) if (dc, dw) != (0, 0)
    ]

    def device(dc, dw):
        return (lax.rem(me + dc, ncells), lax.rem(region + dw, nwells))

    barrier = pltpu.get_barrier_semaphore()
    for dc, dw in peers:
        pl.semaphore_signal(barrier, inc=1, device_id=device(dc, dw), device_id_type=MESH)

    wells, slots = cells_ref.shape
    segs = parent_ref.shape[1]
    rows = state_ref.shape[1]
    shard = rows * LANES
    groups = ncells
    owned = wells // groups
    per = owned * slots // ncells
    total = groups * per
    targets = owned * segs

    offset = cells_ref[...] - me * shard
    inside = (offset >= 0) & (offset < shard)
    mask = ones_where(inside)
    before = ones_where(iota((slots, slots), 0) < iota((slots, slots), 1))
    wi, wj = iota((wells, wells), 0), iota((wells, wells), 1)
    above = ones_where((wi // owned == wj // owned) & (wj < wi))
    full = jnp.ones((slots, slots), BF16)
    rank = dot(mask, before) + dot(dot(above, mask).astype(BF16), full)
    rank = jnp.where(inside, rank, F32(-1.0))
    counts = dot(
        jnp.where(wi == wj, count_ref[...].astype(F32), F32(0.0)).astype(BF16),
        jnp.ones((wells, slots), BF16),
    )
    live = iota((wells, slots), 1).astype(F32) < counts
    weight = jnp.where(live, index_ref[...], F32(0.0))
    hi = jnp.where(inside, offset // LANES, 0).astype(F32)
    lo = jnp.where(inside, offset % LANES, 0).astype(F32)
    slot_seg = iota((1, slots), 1) // (slots // segs)
    parts = (hi, lo) + split3(weight)
    sub = iota((8, slots), 0)
    order = iota((per, slots), 0).astype(F32)
    for g in range(groups):
        feats, picks = [], []
        for j in range(owned):
            w = g * owned + j
            f = jnp.broadcast_to((slot_seg + j * segs).astype(F32), (8, slots))
            for k, part in enumerate(parts):
                f = jnp.where(sub == k, part[w : w + 1], f)
            feats.append(f)
            picks.append(ones_where(rank[w : w + 1] == order))
        feat_scr[:, g * per : (g + 1) * per] = dot_nt(
            jnp.concatenate(feats, axis=1).astype(BF16), jnp.concatenate(picks, axis=1)
        )

    slot_hi = feat_scr[0:1]
    slot_lo = feat_scr[1:2]
    slot_weight = feat_scr[2:3] + feat_scr[3:4] + feat_scr[4:5]
    slot_target = feat_scr[5:6]
    at_lo = ones_where(iota((LANES, total), 0).astype(F32) == slot_lo)
    at_hi = iota((rows, total), 0).astype(F32) == slot_hi
    at_target = ones_where(iota((targets, total), 0).astype(F32) == slot_target)
    in_group = iota((groups, total), 1) // per == iota((groups, total), 0)
    at_lo3 = jnp.concatenate([at_lo] * 3, axis=0)

    def cell_values(values):
        pieces = jnp.concatenate([p.astype(BF16) for p in split3(values)], axis=1)
        spread = dot(pieces, at_lo3)
        return jnp.sum(jnp.where(at_hi, spread, F32(0.0)), axis=0, keepdims=True)

    def table_values(tables):
        pieces = [split3(t) for t in tables]
        stacked = jnp.concatenate([p[i] for i in range(3) for p in pieces], axis=0)
        spread = dot(stacked.astype(BF16), at_target)
        size = len(tables) * groups
        spread = spread[:size] + spread[size : 2 * size] + spread[2 * size :]
        return [
            jnp.sum(
                jnp.where(in_group, spread[k * groups : (k + 1) * groups], F32(0.0)),
                axis=0,
                keepdims=True,
            )
            for k in range(len(tables))
        ]

    def fold(read, scratch):
        for j in range(owned):
            scratch[:, j * segs : (j + 1) * segs] = read(pl.ds(j, groups, stride=owned))
        return scratch[...]

    seg_state = [
        fold(lambda s, k=k: segstate_ref[k, s, :], fold_scr.at[k]) for k in range(3)
    ]
    source = [fold(lambda s, k=k: source_ref[k, s, :], fold_scr.at[3 + k]) for k in range(3)]
    cond = fold(lambda s: cond_ref[s, :], fold_scr.at[6])
    parent = fold(lambda s: parent_ref[s, :], fold_int)

    state_at = [cell_values(state_ref[k]) for k in range(3)]
    jac = [cell_values(jac_ref[k]) for k in range(9)]
    differ = [a - b for a, b in zip(state_at, table_values(seg_state))]
    kmat = []
    for a in range(3):
        for b in range(a, 3):
            entry = sum(jac[3 * a + c] * jac[3 * b + c] for c in range(3))
            kmat.append((entry + 1.0 if a == b else entry) * slot_weight)
    flow = apply3(kmat, differ)
    values = [split3(v) for v in kmat + list(flow)]
    placed = jnp.concatenate(
        [jnp.where(in_group, v[i], F32(0.0)) for i in range(3) for v in values], axis=0
    )
    summed = dot_nt(placed.astype(BF16), at_target)
    size = 9 * groups
    send_buf[...] = summed[:size] + summed[size : 2 * size] + summed[2 * size :]

    pl.semaphore_wait(barrier, len(peers))
    copies = []
    for d in range(1, ncells):
        copy = pltpu.make_async_remote_copy(
            src_ref=send_buf,
            dst_ref=recv_buf.at[d - 1],
            send_sem=send_sem.at[d - 1],
            recv_sem=recv_sem.at[d - 1],
            device_id=device(d, 0),
            device_id_type=MESH,
        )
        copy.start()
        copies.append(copy)

    seg = iota((groups, targets), 1) % segs
    dist = seg - parent
    links = [jnp.where((dist == d) & (seg >= 1), cond, F32(0.0)) for d in (1, 2, 3)]

    def roll(x, shift):
        shift = shift % targets
        return pltpu.roll(x, shift, 1) if shift else x

    diagonal = 1.0 + links[0] + links[1] + links[2]
    for d in (1, 2, 3):
        diagonal = diagonal + roll(links[d - 1], -d)

    table = send_buf[...]
    for copy in copies:
        copy.wait_recv()
    for d in range(1, ncells):
        table = table + recv_buf[d - 1]
    table = [table[k * groups : (k + 1) * groups] for k in range(9)]
    for k in (0, 3, 5):
        table[k] = table[k] + diagonal
    for k in range(3):
        table[6 + k] = table[6 + k] + source[k]
    well_top = [jnp.max(jnp.abs(table[6 + k])) for k in range(3)]

    mats = [[roll(table[k], -s) for k in range(6)] for s in range(segs)]
    vecs = [[roll(table[6 + k], -s) for k in range(3)] for s in range(segs)]
    edges = [[roll(link, -s) for link in links] for s in range(segs)]
    inverses, partial = [None] * segs, [None] * segs
    for s in range(segs - 1, -1, -1):
        inverses[s] = invert3(mats[s])
        partial[s] = apply3(inverses[s], vecs[s])
        for d in (1, 2, 3):
            if s - d >= 0:
                c = edges[s][d - 1]
                c2 = c * c
                mats[s - d] = [a - c2 * i for a, i in zip(mats[s - d], inverses[s])]
                vecs[s - d] = [r + c * y for r, y in zip(vecs[s - d], partial[s])]
    found = [partial[0]]
    for s in range(1, segs):
        pull = [
            sum(edges[s][d - 1] * found[s - d][k] for d in (1, 2, 3) if s - d >= 0)
            for k in range(3)
        ]
        found.append([y + x for y, x in zip(partial[s], apply3(inverses[s], pull))])
    solved = []
    for k in range(3):
        out = found[0][k]
        for s in range(1, segs):
            out = jnp.where(seg == s, roll(found[s][k], s), out)
        solved.append(out)

    mine = iota((groups, targets), 0) == me
    for k in range(3):
        row = jnp.sum(jnp.where(mine, solved[k], F32(0.0)), axis=0, keepdims=True)
        for j in range(owned):
            well_ref[k, j : j + 1, :] = row[:, j * segs : (j + 1) * segs]

    delta = apply3(kmat, table_values(solved))
    at_lo_wide = jnp.concatenate([at_lo] * 3, axis=1)
    corrected, tops = [], []
    for k in range(3):
        spread = jnp.concatenate(
            [jnp.where(at_hi, p, F32(0.0)).astype(BF16) for p in split3(delta[k])], axis=1
        )
        fixed = resid_ref[k] - dot_nt(spread, at_lo_wide)
        corrected.append(fixed)
        tops.append(jnp.max(jnp.abs(fixed)))
    tops = tops + well_top

    lane = iota((1, LANES), 1)
    top = jnp.zeros((1, LANES), F32)
    for k in range(6):
        top = jnp.where(lane == k, tops[k], top)
    top_send[...] = top
    sends = []
    for i, (dc, dw) in enumerate(peers):
        copy = pltpu.make_async_remote_copy(
            src_ref=top_send,
            dst_ref=top_recv.at[i],
            send_sem=top_send_sem,
            recv_sem=top_recv_sem,
            device_id=device(dc, dw),
            device_id_type=MESH,
        )
        copy.start()
    steps = []
    for a in range(3):
        steps.append(sum(inv_ref[3 * a + b] * corrected[b] for b in range(3)))
    pltpu.make_async_copy(top_recv, top_recv, top_recv_sem).wait()
    top = jnp.maximum(top, jnp.max(top_recv[...], axis=0))
    scale = 1.0 / jnp.maximum(F32(1.0), top)
    for k in range(3):
        step_ref[k] = steps[k] * scale[:, k : k + 1]
    for k in range(6):
        max_ref[k] = jnp.max(jnp.where(lane == k, top, F32(0.0)))
    for copy in copies:
        copy.wait_send()
    pltpu.make_async_copy(top_recv, top_recv, top_send_sem).wait()


def on_device(ncells, nwells, *args):
    (
        cell_state,
        cell_residual,
        cell_block,
        block_inverse,
        perf_cells,
        perf_count,
        perf_index,
        seg_parent,
        seg_cond,
        seg_state,
        seg_source,
    ) = args
    shard = cell_state.shape[2]
    rows = shard // LANES
    wells, slots = perf_cells.shape[1:]
    segs = seg_parent.shape[2]
    owned = wells // ncells
    total = owned * slots
    targets = owned * segs
    others = ncells * nwells - 1

    def planes(x):
        return x.reshape(x.shape[0], rows, LANES)

    vmem = pl.BlockSpec(memory_space=pltpu.VMEM)
    step, well, top = pl.pallas_call(
        functools.partial(kernel, ncells, nwells),
        out_shape=(
            jax.ShapeDtypeStruct((3, rows, LANES), F32),
            jax.ShapeDtypeStruct((3, owned, segs), F32),
            jax.ShapeDtypeStruct((6,), F32),
        ),
        in_specs=[vmem] * 11,
        out_specs=(vmem, vmem, pl.BlockSpec(memory_space=pltpu.SMEM)),
        scratch_shapes=[
            pltpu.VMEM((8, total), F32),
            pltpu.VMEM((7, ncells, targets), F32),
            pltpu.VMEM((ncells, targets), jnp.int32),
            pltpu.VMEM((9 * ncells, targets), F32),
            pltpu.VMEM((ncells - 1, 9 * ncells, targets), F32),
            pltpu.VMEM((1, LANES), F32),
            pltpu.VMEM((others, 1, LANES), F32),
            pltpu.SemaphoreType.DMA((ncells - 1,)),
            pltpu.SemaphoreType.DMA((ncells - 1,)),
            pltpu.SemaphoreType.DMA,
            pltpu.SemaphoreType.DMA,
        ],
        compiler_params=pltpu.CompilerParams(collective_id=0, has_side_effects=True),
    )(
        planes(cell_state),
        planes(cell_residual),
        planes(cell_block),
        planes(block_inverse),
        perf_cells[0],
        perf_count,
        perf_index[0],
        seg_parent[0],
        seg_cond[0],
        seg_state[:, 0],
        seg_source[:, 0],
    )
    return (step.reshape(3, 1, shard), well[:, None], top)


def solution(mesh):
    in_specs = (
        P(None, "wells", "cells"),
        P(None, "wells", "cells"),
        P(None, "wells", "cells"),
        P(None, "wells", "cells"),
        P("wells", None, None),
        P("wells", None),
        P("wells", None, None),
        P("wells", None, None),
        P("wells", None, None),
        P(None, "wells", None, None),
        P(None, "wells", None, None),
    )
    out_specs = (P(None, "wells", "cells"), P(None, "wells", "cells", None), P())
    return jax.shard_map(
        functools.partial(on_device, mesh.shape["cells"], mesh.shape["wells"]),
        mesh=mesh,
        in_specs=in_specs,
        out_specs=out_specs,
        check_vma=False,
    )
```

time: 273 us -> 23.7 us (0.09)
  other arithmetic: 113 us -> 0 us
  local copies, waits for them, and re-layouts: 81.6 us -> 2.8 us
  blocking collectives: 75.6 us -> 0 us
  Pallas kernels: 0 us -> 20.1 us
    another operation x7 -> x0, other arithmetic: 65.2 us -> none  [the longest x4 35.4 us: solve_wells(): lower = jnp.linalg.cholesky(dense)]
    pmax x1 -> x0, blocking collectives: 39.4 us -> none  [on_device(): cell_top, well_top = lax.pmax((cell_max, well_max), ('cells', 'wells'))]
    gather x3 -> x0, local copies, waits for them, and re-layouts: 32.3 us -> none  [the longest x1 17.5 us: on_device(): state_at = state[:, safe]]
    scatter-add x1 -> x0, other arithmetic: 29.1 us -> none  [on_device(): jnp.zeros((3, shard_cells), jnp.float32).at[:, safe.reshape(-1)]]
    unnamed x1 -> x0, blocking collectives: 27.8 us -> none
    mul x13 -> x0, local copies, waits for them, and re-layouts: 22.7 us -> none  [the longest x6 11.5 us: solve_wells(): matrix[:, :, None, :, None] * eye_comp[None, None, :, None, :]]
    pallas_call x0 -> x1, Pallas kernels: none -> 20.1 us  [on_device(): pl.pallas_call(functools.partial(kernel, ncells, nwells), out_shape=(jax....]
    unnamed x27 -> x7, local copies, waits for them, and re-layouts: 16.8 us -> 2.8 us
where the time goes in v1:
time: 23.7 us; the launch traced here: 23.5 us
  Pallas kernels  20.1 us (85%)
  local copies, waits for them, and re-layouts  2.8 us (12%)
  between operations  0.65 us (3%)
    pallas_call x1, Pallas kernels, on_device(): pl.pallas_call(functools.partial(kernel, ncells, nwells), out_shape=(jax....  20.1 us
    unnamed x7, local copies, waits for them, and re-layouts  2.8 us

profile of v1, /device:TPU:0, one launch (start us, length us, event | category | flops | bytes accessed | tf_op | source)
XLA Modules:
  0.0 23.5 jit_solution(8540277643427689645)
XLA Ops:
  0.6 20.1 %shard_map.130 = (f32[3,128,128]{2,1,0:T(8,128)}, f32[3,4,32]{2,1,0:T(4,128)}, f32[6]{0:T(128)}) custom-call(f32[3,128,128]{2,1,0:T(8,128)} %bitcast.16, f32[3,128,128]{2,1,0:T(8,128)} %bitcast.17, f32[9,128,128]{2,1,0:T(8,128)} %bitcast.14, f32[9,128,128]{2,1,0:T(8,128)} %bitcast.15, s32[32,128]{1,0:T(8,128)} %bitcast.21, s32[1,32]{1,0:T(1,128)} %count_ref.1, ...), custom_call_target="tpu_custom_call" | custom-call | tf_op jit(solution)/shard_map/pallas_call | solution.py:354
  20.7 0.0 copy-start
  20.7 1.6 %copy.21 = f32[3,1,16384]{2,1,0:T(1,128)} copy(f32[3,1,16384]{2,1,0:T(1,128)} %bitcast.18) | data formatting | bytes 393216
  22.3 0.0 copy-done
  22.3 0.0 copy-start.1
  22.3 0.6 %copy.22 = f32[3,1,4,32]{3,2,1,0:T(4,128)} copy(f32[3,1,4,32]{3,2,1,0:T(4,128)S(1)} %bitcast.25) | data formatting | bytes 3072
  22.9 0.1 copy-done.1
  23.0 0.5 %copy.23 = f32[6]{0:T(128)} copy(f32[6]{0:T(128)S(1)} %copy-done.1) | data formatting | bytes 48
Async XLA Ops:
  20.7 1.6 %copy-start = (f32[3,4,32]{2,1,0:T(4,128)S(1)}, f32[3,4,32]{2,1,0:T(4,128)}, u32[]{:S(2)}) copy-start(f32[3,4,32]{2,1,0:T(4,128)} %get-tuple-element.7) | copy-start | bytes 4612
  22.3 0.7 %copy-start.1 = (f32[6]{0:T(128)S(1)}, f32[6]{0:T(128)}, u32[]{:S(2)}) copy-start(f32[6]{0:T(128)} %get-tuple-element.20) | copy-start | bytes 76

commit v2 on v1

--- a/solution.py
+++ b/solution.py
@@ -68,10 +68,10 @@
 def kernel(
     ncells,
     nwells,
-    state_ref,
-    resid_ref,
-    jac_ref,
-    inv_ref,
+    state_hbm,
+    jac_hbm,
+    resid_hbm,
+    inv_hbm,
     cells_ref,
     count_ref,
     index_ref,
@@ -81,7 +81,12 @@
     source_ref,
     step_ref,
     well_ref,
-    max_ref,
+    top_ref,
+    state_ref,
+    jac_ref,
+    resid_ref,
+    inv_ref,
+    load_sem,
     feat_scr,
     fold_scr,
     fold_int,
@@ -94,6 +99,19 @@
     top_send_sem,
     top_recv_sem,
 ):
+    loads = [
+        pltpu.make_async_copy(src, dst, load_sem.at[i])
+        for i, (src, dst) in enumerate(
+            (
+                (state_hbm, state_ref),
+                (jac_hbm, jac_ref),
+                (resid_hbm, resid_ref),
+                (inv_hbm, inv_ref),
+            )
+        )
+    ]
+    for load in loads:
+        load.start()
     me = lax.axis_index("cells")
     region = lax.axis_index("wells")
     peers = [
@@ -104,7 +122,8 @@
         return (lax.rem(me + dc, ncells), lax.rem(region + dw, nwells))
 
     barrier = pltpu.get_barrier_semaphore()
-    for dc, dw in peers:
+    greeted = [(dc, dw) for dc, dw in peers if dc == 0 or dw == 0]
+    for dc, dw in greeted:
         pl.semaphore_signal(barrier, inc=1, device_id=device(dc, dw), device_id_type=MESH)
 
     wells, slots = cells_ref.shape
@@ -193,6 +212,8 @@
     cond = fold(lambda s: cond_ref[s, :], fold_scr.at[6])
     parent = fold(lambda s: parent_ref[s, :], fold_int)
 
+    loads[0].wait()
+    loads[1].wait()
     state_at = [cell_values(state_ref[k]) for k in range(3)]
     jac = [cell_values(jac_ref[k]) for k in range(9)]
     differ = [a - b for a, b in zip(state_at, table_values(seg_state))]
@@ -210,7 +231,7 @@
     size = 9 * groups
     send_buf[...] = summed[:size] + summed[size : 2 * size] + summed[2 * size :]
 
-    pl.semaphore_wait(barrier, len(peers))
+    pl.semaphore_wait(barrier, len(greeted))
     copies = []
     for d in range(1, ncells):
         copy = pltpu.make_async_remote_copy(
@@ -236,6 +257,11 @@
     for d in (1, 2, 3):
         diagonal = diagonal + roll(links[d - 1], -d)
 
+    edges = [[roll(link, -s) for link in links] for s in range(segs)]
+    at_lo_wide = jnp.concatenate([at_lo] * 3, axis=1)
+    loads[2].wait()
+    loads[3].wait()
+
     table = send_buf[...]
     for copy in copies:
         copy.wait_recv()
@@ -250,7 +276,6 @@
 
     mats = [[roll(table[k], -s) for k in range(6)] for s in range(segs)]
     vecs = [[roll(table[6 + k], -s) for k in range(3)] for s in range(segs)]
-    edges = [[roll(link, -s) for link in links] for s in range(segs)]
     inverses, partial = [None] * segs, [None] * segs
     for s in range(segs - 1, -1, -1):
         inverses[s] = invert3(mats[s])
@@ -282,7 +307,6 @@
             well_ref[k, j : j + 1, :] = row[:, j * segs : (j + 1) * segs]
 
     delta = apply3(kmat, table_values(solved))
-    at_lo_wide = jnp.concatenate([at_lo] * 3, axis=1)
     corrected, tops = [], []
     for k in range(3):
         spread = jnp.concatenate(
@@ -309,19 +333,25 @@
             device_id_type=MESH,
         )
         copy.start()
-    steps = []
     for a in range(3):
-        steps.append(sum(inv_ref[3 * a + b] * corrected[b] for b in range(3)))
+        step_ref[a] = sum(inv_ref[3 * a + b] * corrected[b] for b in range(3))
     pltpu.make_async_copy(top_recv, top_recv, top_recv_sem).wait()
     top = jnp.maximum(top, jnp.max(top_recv[...], axis=0))
-    scale = 1.0 / jnp.maximum(F32(1.0), top)
-    for k in range(3):
-        step_ref[k] = steps[k] * scale[:, k : k + 1]
-    for k in range(6):
-        max_ref[k] = jnp.max(jnp.where(lane == k, top, F32(0.0)))
+    top_ref[...] = top
     for copy in copies:
         copy.wait_send()
     pltpu.make_async_copy(top_recv, top_recv, top_send_sem).wait()
+
+
+def finish(step_in, well_in, top_in, step_ref, well_ref, max_ref):
+    top = top_in[...]
+    scale = 1.0 / jnp.maximum(F32(1.0), top)
+    for k in range(3):
+        step_ref[k] = step_in[k] * scale[:, k : k + 1]
+    well_ref[...] = well_in[...]
+    lane = iota(top.shape, 1)
+    for k in range(6):
+        max_ref[k] = jnp.max(jnp.where(lane == k, top, F32(0.0)))
 
 
 def on_device(ncells, nwells, *args):
@@ -351,16 +381,22 @@
         return x.reshape(x.shape[0], rows, LANES)
 
     vmem = pl.BlockSpec(memory_space=pltpu.VMEM)
-    step, well, top = pl.pallas_call(
+    hbm = pl.BlockSpec(memory_space=pltpu.HBM)
+    raw, found, top = pl.pallas_call(
         functools.partial(kernel, ncells, nwells),
         out_shape=(
             jax.ShapeDtypeStruct((3, rows, LANES), F32),
             jax.ShapeDtypeStruct((3, owned, segs), F32),
-            jax.ShapeDtypeStruct((6,), F32),
+            jax.ShapeDtypeStruct((1, LANES), F32),
         ),
-        in_specs=[vmem] * 11,
-        out_specs=(vmem, vmem, pl.BlockSpec(memory_space=pltpu.SMEM)),
+        in_specs=[hbm] * 4 + [vmem] * 7,
+        out_specs=(vmem, vmem, vmem),
         scratch_shapes=[
+            pltpu.VMEM((3, rows, LANES), F32),
+            pltpu.VMEM((9, rows, LANES), F32),
+            pltpu.VMEM((3, rows, LANES), F32),
+            pltpu.VMEM((9, rows, LANES), F32),
+            pltpu.SemaphoreType.DMA((4,)),
             pltpu.VMEM((8, total), F32),
             pltpu.VMEM((7, ncells, targets), F32),
             pltpu.VMEM((ncells, targets), jnp.int32),
@@ -376,8 +412,8 @@
         compiler_params=pltpu.CompilerParams(collective_id=0, has_side_effects=True),
     )(
         planes(cell_state),
+        planes(cell_block),
         planes(cell_residual),
-        planes(cell_block),
         planes(block_inverse),
         perf_cells[0],
         perf_count,
@@ -387,6 +423,16 @@
         seg_state[:, 0],
         seg_source[:, 0],
     )
+    step, well, top = pl.pallas_call(
+        finish,
+        out_shape=(
+            jax.ShapeDtypeStruct((3, rows, LANES), F32),
+            jax.ShapeDtypeStruct((3, owned, segs), F32),
+            jax.ShapeDtypeStruct((6,), F32),
+        ),
+        in_specs=[vmem] * 3,
+        out_specs=(vmem, vmem, pl.BlockSpec(memory_space=pltpu.SMEM)),
+    )(raw, found, top)
     return (step.reshape(3, 1, shard), well[:, None], top)
 
 

time: 23.7 us -> 22 us (0.928)
  local copies, waits for them, and re-layouts: 2.8 us -> 0 us
  Pallas kernels: 20.1 us -> 21.1 us
    unnamed x7 -> x0, local copies, waits for them, and re-layouts: 2.8 us -> none
    pallas_call x0 -> x1, Pallas kernels: none -> 1.75 us  [on_device(): pl.pallas_call(finish, out_shape=(jax.ShapeDtypeStruct((3, rows, LANES),...]
    pallas_call x1, Pallas kernels: 20.1 us -> 19.4 us  [on_device(): pl.pallas_call(functools.partial(kernel, ncells, nwells), out_shape=(jax....]
where the time goes in v2:
time: 22 us; the launch traced here: 21.8 us
  Pallas kernels  21.1 us (96%)
  between operations  0.64 us (3%)
    pallas_call x1, Pallas kernels, on_device(): pl.pallas_call(functools.partial(kernel, ncells, nwells), out_shape=(jax....  19.4 us
    pallas_call x1, Pallas kernels, on_device(): pl.pallas_call(finish, out_shape=(jax.ShapeDtypeStruct((3, rows, LANES),...  1.75 us

profile of v2, /device:TPU:0, one launch (start us, length us, event | category | flops | bytes accessed | tf_op | source)
XLA Modules:
  0.0 21.8 jit_solution(1527748366625632829)
XLA Ops:
  0.6 19.4 %shard_map.130 = (f32[3,128,128]{2,1,0:T(8,128)}, f32[3,4,32]{2,1,0:T(4,128)}, f32[1,128]{1,0:T(1,128)}) custom-call(f32[3,128,128]{2,1,0:T(8,128)} %bitcast.16, f32[9,128,128]{2,1,0:T(8,128)} %bitcast.14, f32[3,128,128]{2,1,0:T(8,128)} %bitcast.17, f32[9,128,128]{2,1,0:T(8,128)} %bitcast.15, s32[32,128]{1,0:T(8,128)} %bitcast.20, s32[1,32]{1,0:T(1,128)} %count_ref.1, ...), custom_call_target="tpu_custom_call" | custom-call | tf_op jit(solution)/shard_map/pallas_call | solution.py:385
  20.0 1.8 %shard_map.131 = (f32[3,128,128]{2,1,0:T(8,128)}, f32[3,4,32]{2,1,0:T(4,128)}, f32[6]{0:T(128)}) custom-call(f32[3,128,128]{2,1,0:T(8,128)} %get-tuple-element.9.step_in, f32[3,4,32]{2,1,0:T(4,128)} %get-tuple-element.10.well_in, f32[1,128]{1,0:T(1,128)} %get-tuple-element.11.top_in), custom_call_target="tpu_custom_call" | custom-call | tf_op jit(solution)/shard_map/pallas_call | solution.py:426

commit v3 on v2

--- a/solution.py
+++ b/solution.py
@@ -288,8 +288,11 @@
                 vecs[s - d] = [r + c * y for r, y in zip(vecs[s - d], partial[s])]
     found = [partial[0]]
     for s in range(1, segs):
+        near = [d for d in (3, 2, 1) if s - d >= 0]
         pull = [
-            sum(edges[s][d - 1] * found[s - d][k] for d in (1, 2, 3) if s - d >= 0)
+            functools.reduce(
+                lambda a, b: a + b, [edges[s][d - 1] * found[s - d][k] for d in near]
+            )
             for k in range(3)
         ]
         found.append([y + x for y, x in zip(partial[s], apply3(inverses[s], pull))])
@@ -385,9 +388,9 @@
     raw, found, top = pl.pallas_call(
         functools.partial(kernel, ncells, nwells),
         out_shape=(
-            jax.ShapeDtypeStruct((3, rows, LANES), F32),
-            jax.ShapeDtypeStruct((3, owned, segs), F32),
-            jax.ShapeDtypeStruct((1, LANES), F32),
+            pltpu.VMEM((3, rows, LANES), F32),
+            pltpu.VMEM((3, owned, segs), F32),
+            pltpu.VMEM((1, LANES), F32),
         ),
         in_specs=[hbm] * 4 + [vmem] * 7,
         out_specs=(vmem, vmem, vmem),
@@ -432,7 +435,7 @@
         ),
         in_specs=[vmem] * 3,
         out_specs=(vmem, vmem, pl.BlockSpec(memory_space=pltpu.SMEM)),
-    )(raw, found, top)
+    )(*[pltpu.with_memory_space_constraint(x, pltpu.VMEM) for x in (raw, found, top)])
     return (step.reshape(3, 1, shard), well[:, None], top)
 
 

time: 22 us -> 20.3 us (0.923)
  Pallas kernels: 21.1 us -> 19.5 us
    pallas_call x1, Pallas kernels: 1.75 us -> 0.81 us  [on_device(): pl.pallas_call(finish, out_shape=(jax.ShapeDtypeStruct((3, rows, LANES),...]
    pallas_call x1, Pallas kernels: 19.4 us -> 18.7 us  [on_device(): pl.pallas_call(functools.partial(kernel, ncells, nwells), out_shape=(pltp...]
where the time goes in v3:
time: 20.3 us; the launch traced here: 20.1 us
  Pallas kernels  19.5 us (96%)
  between operations  0.64 us (3%)
    pallas_call x1, Pallas kernels, on_device(): pl.pallas_call(functools.partial(kernel, ncells, nwells), out_shape=(pltp...  18.7 us
    pallas_call x1, Pallas kernels, on_device(): pl.pallas_call(finish, out_shape=(jax.ShapeDtypeStruct((3, rows, LANES),...  0.81 us

profile of v3, /device:TPU:0, one launch (start us, length us, event | category | flops | bytes accessed | tf_op | source)
XLA Modules:
  0.0 20.1 jit_solution(13562767011875731926)
XLA Ops:
  0.6 18.7 %shard_map.130 = (f32[3,128,128]{2,1,0:T(8,128)S(1)}, f32[3,4,32]{2,1,0:T(4,128)S(1)}, f32[1,128]{1,0:T(1,128)S(1)}) custom-call(f32[3,128,128]{2,1,0:T(8,128)} %bitcast.16, f32[9,128,128]{2,1,0:T(8,128)} %bitcast.14, f32[3,128,128]{2,1,0:T(8,128)} %bitcast.17, f32[9,128,128]{2,1,0:T(8,128)} %bitcast.15, s32[32,128]{1,0:T(8,128)} %bitcast.20, ...), custom_call_target="tpu_custom_call" | custom-call | tf_op jit(solution)/shard_map/pallas_call | solution.py:388
  19.3 0.8 %shard_map.131 = (f32[3,128,128]{2,1,0:T(8,128)}, f32[3,4,32]{2,1,0:T(4,128)}, f32[6]{0:T(128)}) custom-call(f32[3,128,128]{2,1,0:T(8,128)S(1)} %get-tuple-element.9.step_in, f32[3,4,32]{2,1,0:T(4,128)S(1)} %get-tuple-element.10.well_in, f32[1,128]{1,0:T(1,128)S(1)} %get-tuple-element.11.top_in), custom_call_target="tpu_custom_call" | custom-call | tf_op jit(solution)/shard_map/pallas_call | solution.py:429

commit v4 on v3

--- a/solution.py
+++ b/solution.py
@@ -36,15 +36,18 @@
     return jnp.where(cond, F32(1.0), F32(0.0)).astype(BF16)
 
 
+def most(x):
+    return jnp.max(jnp.max(jnp.abs(x), axis=0, keepdims=True), axis=1, keepdims=True)
+
+
 def invert3(a):
     a00, a01, a02, a11, a12, a22 = a
     q0 = 1.0 / a00
     l1 = a01 * q0
     l2 = a02 * q0
-    b11 = a11 - l1 * a01
     b12 = a12 - l1 * a02
     b22 = a22 - l2 * a02
-    q1 = 1.0 / b11
+    q1 = a00 * (1.0 / (a00 * a11 - a01 * a01))
     m = b12 * q1
     i22 = 1.0 / (b22 - m * b12)
     i12 = -m * i22
@@ -272,7 +275,7 @@
         table[k] = table[k] + diagonal
     for k in range(3):
         table[6 + k] = table[6 + k] + source[k]
-    well_top = [jnp.max(jnp.abs(table[6 + k])) for k in range(3)]
+    well_top = [most(table[6 + k]) for k in range(3)]
 
     mats = [[roll(table[k], -s) for k in range(6)] for s in range(segs)]
     vecs = [[roll(table[6 + k], -s) for k in range(3)] for s in range(segs)]
@@ -317,7 +320,7 @@
         )
         fixed = resid_ref[k] - dot_nt(spread, at_lo_wide)
         corrected.append(fixed)
-        tops.append(jnp.max(jnp.abs(fixed)))
+        tops.append(most(fixed))
     tops = tops + well_top
 
     lane = iota((1, LANES), 1)

time: 20.3 us -> 20.1 us (level)
    pallas_call x1, Pallas kernels: 18.7 us -> 18.5 us  [on_device(): pl.pallas_call(functools.partial(kernel, ncells, nwells), out_shape=(pltp...]
where the time goes in v4:
time: 20.1 us; the launch traced here: 19.9 us
  Pallas kernels  19.3 us (96%)
  between operations  0.64 us (3%)
    pallas_call x1, Pallas kernels, on_device(): pl.pallas_call(functools.partial(kernel, ncells, nwells), out_shape=(pltp...  18.5 us
    pallas_call x1, Pallas kernels, on_device(): pl.pallas_call(finish, out_shape=(jax.ShapeDtypeStruct((3, rows, LANES),...  0.81 us

profile of v4, /device:TPU:0, one launch (start us, length us, event | category | flops | bytes accessed | tf_op | source)
XLA Modules:
  0.0 19.9 jit_solution(7715802541476706974)
XLA Ops:
  0.6 18.5 %shard_map.130 = (f32[3,128,128]{2,1,0:T(8,128)S(1)}, f32[3,4,32]{2,1,0:T(4,128)S(1)}, f32[1,128]{1,0:T(1,128)S(1)}) custom-call(f32[3,128,128]{2,1,0:T(8,128)} %bitcast.16, f32[9,128,128]{2,1,0:T(8,128)} %bitcast.14, f32[3,128,128]{2,1,0:T(8,128)} %bitcast.17, f32[9,128,128]{2,1,0:T(8,128)} %bitcast.15, s32[32,128]{1,0:T(8,128)} %bitcast.20, ...), custom_call_target="tpu_custom_call" | custom-call | tf_op jit(solution)/shard_map/pallas_call | solution.py:391
  19.1 0.8 %shard_map.131 = (f32[3,128,128]{2,1,0:T(8,128)}, f32[3,4,32]{2,1,0:T(4,128)}, f32[6]{0:T(128)}) custom-call(f32[3,128,128]{2,1,0:T(8,128)S(1)} %get-tuple-element.9.step_in, f32[3,4,32]{2,1,0:T(4,128)S(1)} %get-tuple-element.10.well_in, f32[1,128]{1,0:T(1,128)S(1)} %get-tuple-element.11.top_in), custom_call_target="tpu_custom_call" | custom-call | tf_op jit(solution)/shard_map/pallas_call | solution.py:432
